TPU v7x, 256 devices: a 2x2x32 block of a 4x8x32 slice. The times are simulated.
256 devices in a mesh: grp: 4 (over y, x), freq: 64 (over z, core).
Axes of the slice: x: 2, y: 2, z: 32, core: 2. Of those that a mesh axis runs over, the one named last changes fastest.
The devices are a block of a 4x8x32 slice.
Arguments:
- kernel: bfloat16 [2, 512, 1024, 1024], P(None, ('grp', 'freq')), parts along dimension 1, may hold values from -0.125 to 0.125
- recorded: float32 [2, 512, 1024, 128], P(None, ('grp', 'freq')), parts along dimension 1, may hold values from -8 to 8
- onset_time: int32 [4096, 128], P(('grp', 'freq')), parts along dimension 0, may hold values from 32 to 256, as said below
Outputs:
- focusing: float32 [256, 4096, 128], P(None, ('grp', 'freq')), parts along dimension 1
There are 4 independent parts, one for each index of `grp`. A program takes and returns all parts, laid end to end along the dimension named above; each array names one. Nothing has to cross between parts.
Inputs may be any that keep to these rules, and one draw needn't show every extreme that they name: `onset_time`: onset sample of the window for each receiver and focal point.
All inputs are finite; a program needn't handle non-finite values.
Results may differ from a plain program's by a relative error of at most 0.012.
Values may be sent and summed in bfloat16 or wider, within the bound.
A program may use at most 64 MiB of HBM per device.

v0:
```python
import functools
import math

import jax
import jax.numpy as jnp
from jax import lax
from jax.sharding import Mesh
from jax.sharding import PartitionSpec as P

NF = 128
ITERS = 2
FREQ = ("freq_0", "freq_1")
GRP_FREQ = ("grp", "freq_0", "freq_1")


def by_axis(shard, axes):
    return functools.reduce(lax.psum, axes, shard)


def dft_tables():
    samples = jnp.arange(2 * NF, dtype=jnp.int32)
    bins = jnp.arange(NF, dtype=jnp.int32)
    phase = (bins[:, None] * samples[None, :] % (2 * NF)).astype(jnp.float32) * (math.pi / NF)
    factor = 1.0 / math.sqrt(NF)
    return (jnp.cos(phase) * factor, jnp.sin(phase) * factor)


def square_sum(values):
    return jnp.sum(values * values)


def joint_total(first, second, third):
    return (by_axis(first, FREQ), by_axis(second, FREQ), by_axis(third, FREQ))


def body(kernel, recorded, onset_time):
    cosine_table, sin_tab = dft_tables()
    rec_local = onset_time.shape[0]
    focal_count = onset_time.shape[1]
    samples = lax.broadcasted_iota(jnp.int32, (2 * NF, rec_local, focal_count), 0)
    keep_mask = (samples < onset_time[None]).astype(jnp.float32)
    kernel_real = kernel[0]
    kernel_imaginary = kernel[1]

    def invert(block_in):
        columns = block_in.shape[3]
        widened = block_in.astype(jnp.float32)
        timed = jnp.dot(cosine_table.T, widened[0].reshape(NF, -1)) - jnp.dot(
            sin_tab.T, widened[1].reshape(NF, -1)
        )
        return timed.reshape(2 * NF, block_in.shape[2], columns)

    def apply_adjoint(resid):
        rounded = resid.astype(jnp.bfloat16)
        update_real = rounded[0]
        update_imaginary = rounded[1]
        z_real = jnp.einsum(
            "hvi,hvg->hig", kernel_real, update_real, preferred_element_type=jnp.float32
        ) + jnp.einsum(
            "hvi,hvg->hig", kernel_imaginary, update_imaginary, preferred_element_type=jnp.float32
        )
        z_imag = jnp.einsum(
            "hvi,hvg->hig", kernel_real, update_imaginary, preferred_element_type=jnp.float32
        ) - jnp.einsum(
            "hvi,hvg->hig", kernel_imaginary, update_real, preferred_element_type=jnp.float32
        )
        image = jnp.stack([z_real, z_imag]).astype(jnp.bfloat16)
        timed = invert(lax.all_to_all(image, FREQ, split_axis=2, concat_axis=1, tiled=True))
        return timed * keep_mask

    model_raw = apply_adjoint(recorded)
    totals = joint_total(square_sum(recorded), square_sum(model_raw), jnp.float32(0.0))
    beta_now = jnp.sqrt(totals[0])
    data_vec = recorded / beta_now
    alpha_now = jnp.sqrt(totals[1]) / beta_now
    model_vec = model_raw / (alpha_now * beta_now)
    search = model_vec
    estimate = jnp.zeros_like(model_vec)
    phibar_now = beta_now
    rhobar_now = alpha_now
    for iteration in range(ITERS):
        flat_part = (model_vec * keep_mask).reshape(2 * NF, -1)
        spec_real = jnp.dot(cosine_table, flat_part)
        spec_imag = -jnp.dot(sin_tab, flat_part)
        spectrum = (
            jnp.stack([spec_real, spec_imag])
            .reshape(2, NF, rec_local, focal_count)
            .astype(jnp.bfloat16)
        )
        multiply_block_in = lax.all_to_all(spectrum, FREQ, split_axis=1, concat_axis=2, tiled=True)
        solution_real = multiply_block_in[0]
        solution_imaginary = multiply_block_in[1]
        y_real = jnp.einsum(
            "ptx,pxi->pti", kernel_real, solution_real, preferred_element_type=jnp.float32
        ) - jnp.einsum(
            "ptx,pxi->pti", kernel_imaginary, solution_imaginary, preferred_element_type=jnp.float32
        )
        y_imag = jnp.einsum(
            "ptx,pxi->pti", kernel_real, solution_imaginary, preferred_element_type=jnp.float32
        ) + jnp.einsum(
            "ptx,pxi->pti", kernel_imaginary, solution_real, preferred_element_type=jnp.float32
        )
        data_raw = jnp.stack([y_real, y_imag]) - alpha_now * data_vec
        image_raw = apply_adjoint(data_raw)
        totals = joint_total(
            square_sum(data_raw), square_sum(image_raw), jnp.sum(image_raw * model_vec)
        )
        beta_now = jnp.sqrt(totals[0])
        data_vec = data_raw / beta_now
        alpha_now = jnp.sqrt(
            totals[1] / (beta_now * beta_now) - 2.0 * totals[2] + beta_now * beta_now
        )
        model_vec = (image_raw / beta_now - beta_now * model_vec) / alpha_now
        rho_now = jnp.sqrt(rhobar_now * rhobar_now + beta_now * beta_now)
        cosine = rhobar_now / rho_now
        sine_part = beta_now / rho_now
        theta_now = sine_part * alpha_now
        rhobar_now = -cosine * alpha_now
        phi_now = cosine * phibar_now
        phibar_now = sine_part * phibar_now
        estimate = estimate + phi_now / rho_now * search
        search = model_vec - theta_now / rho_now * search
    return estimate


def solution(mesh):
    torus = Mesh(mesh.devices.reshape(mesh.shape["grp"], 32, 2), ("grp", "freq_0", "freq_1"))
    placed = (P(None, GRP_FREQ, None, None), P(None, GRP_FREQ, None, None), P(GRP_FREQ, None))
    return jax.shard_map(
        body, mesh=torus, in_specs=placed, out_specs=P(None, GRP_FREQ, None), check_vma=False
    )
```

profile of v0, /device:TPU:37, one launch (start us, length us, event | category | flops | bytes accessed | tf_op | source)
XLA Modules:
  0.0 738.9 jit_solution(18064123041767849132)
XLA Ops:
  0.0 3.5 multiply_reduce_fusion.3
  3.5 4.0 fusion.14
  7.6 1.8 fusion.12
  9.4 1.6 fusion.101
  11.0 1.8 fusion.104
  12.9 1.1 copy.81
  14.0 142.1 %all_to_all.60 = bf16[2,2,1024,128]{3,1,0,2:T(2,128)(2,1)S(1)} all-to-all(bf16[2,2,1024,128]{3,1,0,2:T(2,128)(2,1)S(1)} %copy.81), channel_id=1, replica_groups=mesh['grp'=4,'freq_0'=32,'freq_1'=2] {'freq_0','freq_1'}, dimensions={2} | all-to-all | bytes 2097152 | tf_op jit(solution)/shard_map/all_to_all | solution.py:68
  156.4 0.9 fusion.142
  157.3 1.8 multiply_reduce_fusion.4
  159.1 41.1 %all-reduce.1 = (f32[]{:T(128)}, f32[]{:T(128)}) all-reduce(f32[]{:T(128)} %get-tuple-element.29, f32[]{:T(128)} %get-tuple-element.19), channel_id=1, replica_groups=mesh['grp'=4,'freq_0'=32,'freq_1'=2] {'freq_0'}, use_global_device_ids=true, to_apply=%region_1.2 | all-reduce | flops 2 | bytes 16 | tf_op jit(solution)/shard_map/psum | solution.py:17
  200.2 18.1 %all-reduce.3 = (f32[]{:T(128)}, f32[]{:T(128)}) all-reduce(f32[]{:T(128)} %get-tuple-element.10, f32[]{:T(128)} %get-tuple-element.11), channel_id=1, replica_groups=mesh['grp'=4,'freq_0'=32,'freq_1'=2] {'freq_1'}, use_global_device_ids=true, to_apply=%region_2.3 | all-reduce | flops 2 | bytes 16 | tf_op jit(solution)/shard_map/psum | solution.py:17
  219.7 1.0 fusion.109
  220.7 1.0 fusion.112
  222.1 1.1 pad_maximum_fusion.1
  223.2 7.9 %all-to-all-start.1 = ((bf16[2,128,16,128]{3,2,0,1:T(8,128)(2,1)}), bf16[2,128,16,128]{3,2,0,1:T(8,128)(2,1)S(1)}, u32[]{:S(2)}, u32[]{:S(2)}) async-start(bf16[2,128,16,128]{3,2,0,1:T(8,128)(2,1)} %pad_maximum_fusion.1), calls=%async_computation.1 | async-start | bytes 2097152 | tf_op jit(solution)/shard_map/all_to_all | solution.py:90
  231.2 2.9 copy.96
  234.0 104.1 %all-to-all-done.1 = bf16[2,128,16,128]{3,2,0,1:T(8,128)(2,1)S(1)} async-done(((bf16[2,128,16,128]{3,2,0,1:T(8,128)(2,1)}), bf16[2,128,16,128]{3,2,0,1:T(8,128)(2,1)S(1)}, u32[]{:S(2)}, u32[]{:S(2)}) %all-to-all-start.1) | async-done | bytes 1048608 | tf_op jit(solution)/shard_map/all_to_all | solution.py:90
  338.5 3.8 fusion.10
  342.4 3.7 fusion.8
  346.2 1.5 fusion.56
  347.7 1.5 fusion.62
  349.3 1.2 multiply_reduce_fusion.2
  350.6 0.7 fusion.6
  351.8 0.7 fusion.4
  352.6 0.8 fusion.95
  353.3 0.7 fusion.98
  354.2 2.0 copy.101
  356.2 116.7 %all_to_all.61 = bf16[2,2,1024,128]{3,1,0,2:T(2,128)(2,1)S(1)} all-to-all(bf16[2,2,1024,128]{3,1,0,2:T(2,128)(2,1)} %copy.101), channel_id=1, replica_groups=mesh['grp'=4,'freq_0'=32,'freq_1'=2] {'freq_0','freq_1'}, dimensions={2} | all-to-all | bytes 2097152 | tf_op jit(solution)/shard_map/all_to_all | solution.py:68
  473.3 0.9 fusion.137
  474.3 3.3 multiply_reduce_fusion
  477.6 39.7 %all-reduce = (f32[]{:T(128)}, f32[]{:T(128)}, f32[]{:T(128)}) all-reduce(f32[]{:T(128)} %get-tuple-element.17, f32[]{:T(128)} %get-tuple-element.6, f32[]{:T(128)} %get-tuple-element.5), channel_id=1, replica_groups=mesh['grp'=4,'freq_0'=32,'freq_1'=2] {'freq_0'}, use_global_device_ids=true, to_apply=%region_7.8 | all-reduce | flops 3 | bytes 24 | tf_op jit(solution)/shard_map/psum | solution.py:17
  517.3 19.5 %all-reduce.2 = (f32[]{:T(128)}, f32[]{:T(128)}, f32[]{:T(128)}) all-reduce(f32[]{:T(128)} %get-tuple-element.7, f32[]{:T(128)} %get-tuple-element.8, f32[]{:T(128)} %get-tuple-element.9), channel_id=1, replica_groups=mesh['grp'=4,'freq_0'=32,'freq_1'=2] {'freq_1'}, use_global_device_ids=true, to_apply=%region_8.9 | all-reduce | flops 3 | bytes 24 | tf_op jit(solution)/shard_map/psum | solution.py:17
  538.7 2.4 divide_select_fusion
  541.0 0.8 fusion.108
  541.8 0.8 fusion.107
  542.9 1.1 pad_maximum_fusion.3
  544.0 7.9 %all-to-all-start.3 = ((bf16[2,128,16,128]{3,2,0,1:T(8,128)(2,1)}), bf16[2,128,16,128]{3,2,0,1:T(8,128)(2,1)S(1)}, u32[]{:S(2)}, u32[]{:S(2)}) async-start(bf16[2,128,16,128]{3,2,0,1:T(8,128)(2,1)} %pad_maximum_fusion.3), calls=%async_computation.3 | async-start | bytes 2097152 | tf_op jit(solution)/shard_map/all_to_all | solution.py:90
  551.9 1.7 copy.144
  553.8 105.1 %all-to-all-done.3 = bf16[2,128,16,128]{3,2,0,1:T(8,128)(2,1)S(1)} async-done(((bf16[2,128,16,128]{3,2,0,1:T(8,128)(2,1)}), bf16[2,128,16,128]{3,2,0,1:T(8,128)(2,1)S(1)}, u32[]{:S(2)}, u32[]{:S(2)}) %all-to-all-start.3) | async-done | bytes 1048608 | tf_op jit(solution)/shard_map/all_to_all | solution.py:90
  659.3 3.8 fusion.2
  663.2 3.7 fusion
  667.0 1.5 fusion.74
  668.5 1.5 fusion.80
  670.1 1.2 fusion.40
  671.3 41.0 %psum.94 = f32[]{:T(128)} all-reduce(f32[]{:T(128)} %fusion.40), channel_id=1, replica_groups=mesh['grp'=4,'freq_0'=32,'freq_1'=2] {'freq_0'}, use_global_device_ids=true, to_apply=%region_16.17 | all-reduce | flops 1 | bytes 8 | tf_op jit(solution)/shard_map/psum | solution.py:17
  712.4 3.5 copy.149
  715.9 18.1 %psum.95 = f32[]{:T(128)} all-reduce(f32[]{:T(128)} %psum.94), channel_id=1, replica_groups=mesh['grp'=4,'freq_0'=32,'freq_1'=2] {'freq_1'}, use_global_device_ids=true, to_apply=%region_17.18 | all-reduce | flops 1 | bytes 8 | tf_op jit(solution)/shard_map/psum | solution.py:17
  734.8 3.8 multiply_add_fusion
  (46 shorter events, 3.1 us)
Async XLA Ops:
  0.0 7.6 %copy-start = (bf16[2,2,1024,1024]{3,2,1,0:T(8,128)(2,1)S(1)}, bf16[2,2,1024,1024]{3,2,1,0:T(8,128)(2,1)}, u32[]{:S(2)}) copy-start(bf16[2,2,1024,1024]{3,2,1,0:T(8,128)(2,1)} %param.3) | copy-start | bytes 25165828
  156.2 1.1 copy-start.5
  223.2 114.9 %all-to-all-start.1 = ((bf16[2,128,16,128]{3,2,0,1:T(8,128)(2,1)}), bf16[2,128,16,128]{3,2,0,1:T(8,128)(2,1)S(1)}, u32[]{:S(2)}, u32[]{:S(2)}) async-start(bf16[2,128,16,128]{3,2,0,1:T(8,128)(2,1)} %pad_maximum_fusion.1), calls=%async_computation.1 | async-start | bytes 2097152 | tf_op jit(solution)/shard_map/all_to_all | solution.py:90
  338.3 7.8 %slice-start = ((s8[8388608]{0:T(1024)(128)(4,1)}), s8[4194304]{0:T(1024)(128)(4,1)S(1)}, s32[]{:S(2)}) async-start(s8[8388608]{0:T(1024)(128)(4,1)} %bitcast.237), calls=%async_computation.4 | async-start | bytes 8388608
  338.5 7.6 %slice-start.1 = ((s8[8388608]{0:T(1024)(128)(4,1)}), s8[4194304]{0:T(1024)(128)(4,1)S(1)}, s32[]{:S(2)}) async-start(s8[8388608]{0:T(1024)(128)(4,1)} %bitcast.237), calls=%async_computation.5 | async-start | bytes 8388608
  347.7 1.6 copy-start.4
  350.5 1.4 copy-start.1
  544.0 114.9 %all-to-all-start.3 = ((bf16[2,128,16,128]{3,2,0,1:T(8,128)(2,1)}), bf16[2,128,16,128]{3,2,0,1:T(8,128)(2,1)S(1)}, u32[]{:S(2)}, u32[]{:S(2)}) async-start(bf16[2,128,16,128]{3,2,0,1:T(8,128)(2,1)} %pad_maximum_fusion.3), calls=%async_computation.3 | async-start | bytes 2097152 | tf_op jit(solution)/shard_map/all_to_all | solution.py:90
  659.1 7.8 %slice-start.2 = ((s8[8388608]{0:T(1024)(128)(4,1)}), s8[4194304]{0:T(1024)(128)(4,1)S(1)}, s32[]{:S(2)}) async-start(s8[8388608]{0:T(1024)(128)(4,1)} %bitcast.239), calls=%async_computation.6 | async-start | bytes 8388608
  659.3 7.6 %slice-start.3 = ((s8[8388608]{0:T(1024)(128)(4,1)}), s8[4194304]{0:T(1024)(128)(4,1)S(1)}, s32[]{:S(2)}) async-start(s8[8388608]{0:T(1024)(128)(4,1)} %bitcast.239), calls=%async_computation.7 | async-start | bytes 8388608
  668.5 1.6 copy-start.2
  712.4 22.4 %copy-start.3 = (f32[32,8,16,128]{3,2,1,0:T(8,128)S(1)}, f32[32,8,16,128]{3,2,1,0:T(8,128)}, u32[]{:S(2)}) copy-start(f32[32,8,16,128]{3,2,1,0:T(8,128)} %copy.144) | copy-start | bytes 6291460
where the time goes:
time: 747 us; the launch traced here: 739 us
  blocking collectives  436 us (58%)
  waiting for transfers between devices  209 us (28%)
  matrix products  43.9 us (6%)
  starting transfers between devices  15.9 us (2%)
  other arithmetic  14.6 us (2%)
  local copies, waits for them, and re-layouts  13.9 us (2%)
    all_to_all x2, blocking collectives, apply_adjoint(): lax.all_to_all(image, FREQ, split_axis=2, concat_axis=1, tiled=True)  259 us
    all_to_all x2, waiting for transfers between devices, body(): lax.all_to_all(spectrum, FREQ, split_axis=1, concat_axis=2, tiled=True)  209 us
    psum x6, blocking collectives, by_axis(): return functools.reduce(lax.psum, axes, shard)  178 us
    all_to_all x2, starting transfers between devices, body(): lax.all_to_all(spectrum, FREQ, split_axis=1, concat_axis=2, tiled=True)  15.9 us
  transfers between devices with their start and end apart: 2, of which 2 were waited for; matrix products, arithmetic and copies ran while one was open for 1% of the time, Pallas kernels for 0%

commit v1 on v0

v1 whole, which is shorter than its diff:
```python
import functools

import jax
import jax.numpy as jnp
import numpy as np
from jax import lax
from jax.experimental import pallas as pl
from jax.experimental.pallas import tpu as pltpu
from jax.sharding import PartitionSpec as P

CORES = 2
HALF = 8
MIB = 2**20
MESH = pl.DeviceIdType.MESH
F32 = jnp.float32
BF16 = jnp.bfloat16


def dft_tables(bins):
    samples = 2 * bins
    phase = np.outer(np.arange(bins), np.arange(samples)) % samples * (np.pi / bins)
    scale = 1.0 / np.sqrt(bins)
    both = np.concatenate([np.cos(phase) * scale, -np.sin(phase) * scale], axis=0)
    return both.astype(jnp.bfloat16)


def dot(left, right):
    return jnp.dot(left, right, preferred_element_type=F32)


def body(
    group,
    kern_hbm,
    data_hbm,
    onset,
    to_freq,
    to_time,
    out,
    kern,
    kern_t,
    data,
    resid,
    weights,
    model,
    field,
    image_out,
    image_in,
    spec_out,
    spec_in,
    wide,
    sums_out,
    sums_in,
    load_sem,
    send_sem,
    recv_sem,
    own_sem,
    sum_send,
    sum_recv,
):
    me = lax.axis_index("freq")
    chips = group // CORES
    chip = me // CORES
    core = lax.rem(me, CORES)
    nf = kern.shape[1]
    src = kern.shape[2]
    rec = kern.shape[3]
    focal = onset.shape[1]
    bins = group * nf
    samples = 2 * bins

    def peer(chip_step, core_step):
        return lax.rem(chip + chip_step + chips, chips) * CORES + lax.rem(core + core_step, CORES)

    def for_peers(act):
        far = chips // 2
        for other in range(CORES):
            act(peer(far, other))

        def step(i, carry):
            d = far - 1 - i
            for other in range(CORES):
                act(peer(d, other))
                act(peer(-d, other))
            return carry

        lax.fori_loop(0, far - 1, step, 0)
        act(peer(0, 1))

    barrier = pltpu.get_barrier_semaphore()
    for_peers(
        lambda p: pl.semaphore_signal(barrier, inc=1, device_id={"freq": p}, device_id_type=MESH)
    )
    loads = []
    for h in range(nf):
        for c in range(2):
            loads.append(pltpu.make_async_copy(data_hbm.at[c, h], data.at[c, h], load_sem.at[0, c, h]))
            loads.append(pltpu.make_async_copy(kern_hbm.at[c, h], kern.at[c, h], load_sem.at[1, c, h]))
    for load in loads:
        load.start()

    def exchange(outgoing, incoming, kind, turn, part):
        send = send_sem.at[kind, turn, part]
        recv = recv_sem.at[kind, turn, part]
        source = outgoing.at[turn, part]
        target = incoming.at[turn, part]

        def push(p):
            pltpu.make_async_remote_copy(
                src_ref=source.at[p],
                dst_ref=target.at[me],
                send_sem=send,
                recv_sem=recv,
                device_id={"freq": p},
                device_id_type=MESH,
            ).start()

        for_peers(push)
        pltpu.make_async_copy(source.at[me], target.at[me], own_sem.at[kind, turn, part]).start()

    def arrived(outgoing, incoming, kind, turn, part):
        source = outgoing.at[turn, part]
        target = incoming.at[turn, part]
        rest = target.at[pl.ds(0, group - 1)]
        pltpu.make_async_copy(rest, rest, recv_sem.at[kind, turn, part]).wait()
        pltpu.make_async_copy(source.at[me], target.at[me], own_sem.at[kind, turn, part]).wait()

    def sent(outgoing, kind, turn, part):
        rest = outgoing.at[turn, part, pl.ds(0, group - 1)]
        pltpu.make_async_copy(rest, rest, send_sem.at[kind, turn, part]).wait()

    lane = lax.broadcasted_iota(jnp.int32, (1, 128), 1)

    def share(slot, values):
        row = jnp.zeros((1, 128), F32)
        for i, value in enumerate(values):
            row = jnp.where(lane == i, value, row)
        sums_out[slot] = row
        sums_in[slot, me] = row

        def push(p):
            pltpu.make_async_remote_copy(
                src_ref=sums_out.at[slot],
                dst_ref=sums_in.at[slot, me],
                send_sem=sum_send.at[slot],
                recv_sem=sum_recv.at[slot],
                device_id={"freq": p},
                device_id_type=MESH,
            ).start()

        for_peers(push)

    def collect(slot, count):
        rest = sums_in.at[slot, pl.ds(0, group - 1)]
        pltpu.make_async_copy(rest, rest, sum_recv.at[slot]).wait()
        total = jnp.sum(sums_in[slot], axis=0)
        return [jnp.sum(jnp.where(lane == i, total, 0.0), axis=1, keepdims=True) for i in range(count)]

    def full_sum(values):
        return jnp.sum(jnp.sum(values, axis=0, keepdims=True), axis=1, keepdims=True)

    def put_weights(h, rows, real, imag):
        rows_low = pl.ds(src + rows.start, rows.size)
        weights[h, rows, :focal] = real.astype(BF16)
        weights[h, rows, focal:] = imag.astype(BF16)
        weights[h, rows_low, :focal] = imag.astype(BF16)
        weights[h, rows_low, focal:] = (-real).astype(BF16)

    block = 256

    def adjoint(turn):
        for h in range(nf):

            def step(i, carry):
                rows = pl.ds(pl.multiple_of(i * block, block), block)
                got = dot(kern_t[0, h, rows, :], weights[h, :src, :]) + dot(
                    kern_t[1, h, rows, :], weights[h, src:, :]
                )
                owners = block // (2 * HALF)
                real = got[:, :focal].reshape(owners, 2, HALF, focal)
                imag = got[:, focal:].reshape(owners, 2, HALF, focal)
                for part in range(2):
                    image_out[turn, part, pl.ds(i * owners, owners), h] = jnp.concatenate(
                        [real[:, part], imag[:, part]], axis=1
                    ).astype(BF16)
                return carry

            lax.fori_loop(0, rec // block, step, 0)

    def window(turn, part, combine):
        wide[...] = image_in[turn, part].astype(F32).reshape(bins * 2 * HALF, focal)
        norm = jnp.zeros((1, 2 * focal), F32)
        time = lax.broadcasted_iota(jnp.int32, (samples, focal), 0)
        for pair in range(HALF // 2):
            first, second = 2 * pair, 2 * pair + 1

            def column(r):
                return jnp.concatenate(
                    [
                        wide[pl.ds(r, bins, stride=2 * HALF), :],
                        wide[pl.ds(HALF + r, bins, stride=2 * HALF), :],
                    ],
                    axis=0,
                ).astype(BF16)

            timed = dot(to_time[...], jnp.concatenate([column(first), column(second)], axis=1))
            kept = []
            for i, r in enumerate((first, second)):
                row = part * HALF + r
                keep = time < onset[pl.ds(row, 1), :]
                value = jnp.where(keep, timed[:, i * focal : (i + 1) * focal], 0.0)
                kept.append(combine(row, value))
            kept = jnp.concatenate(kept, axis=1)
            norm = norm + jnp.sum(kept * kept, axis=0, keepdims=True)
            spec = dot(to_freq[...], kept.astype(BF16))
            for i, r in enumerate((first, second)):
                cols = slice(i * focal, (i + 1) * focal)
                wide[pl.ds(r, bins, stride=2 * HALF), :] = spec[:bins, cols]
                wide[pl.ds(HALF + r, bins, stride=2 * HALF), :] = spec[bins:, cols]
        spec_out[turn, part] = wide[...].reshape(group, nf, 2 * HALF, focal).astype(BF16)
        return norm

    def forward(turn, finish):
        norm = jnp.zeros((1, 2 * focal), F32)
        for h in range(nf):

            def spread(i, carry):
                owners = 8
                parts = [
                    spec_in[turn, part, pl.ds(i * owners, owners), h].astype(F32) for part in range(2)
                ]
                rows = pl.ds(pl.multiple_of(i * owners * 2 * HALF, 128), owners * 2 * HALF)
                real = jnp.concatenate([p[:, :HALF] for p in parts], axis=1).reshape(-1, focal)
                imag = jnp.concatenate([p[:, HALF:] for p in parts], axis=1).reshape(-1, focal)
                rows_low = pl.ds(pl.multiple_of(rec + i * owners * 2 * HALF, 128), owners * 2 * HALF)
                weights[h, rows, :focal] = real.astype(BF16)
                weights[h, rows, focal:] = imag.astype(BF16)
                weights[h, rows_low, :focal] = (-imag).astype(BF16)
                weights[h, rows_low, focal:] = real.astype(BF16)
                return carry

            lax.fori_loop(0, group // 8, spread, 0)

            def step(i, norm):
                rows = pl.ds(pl.multiple_of(i * block, block), block)
                got = dot(kern[0, h, rows, :], weights[h, :rec, :]) + dot(
                    kern[1, h, rows, :], weights[h, rec:, :]
                )
                value = finish(h, rows, got)
                return norm + jnp.sum(value * value, axis=0, keepdims=True)

            norm = lax.fori_loop(0, src // block, step, norm)
        return full_sum(norm)

    data_norm = jnp.zeros((1, focal), F32)
    for load in loads[0::2]:
        load.wait()
    for h in range(nf):
        for c in range(2):
            data_norm = data_norm + jnp.sum(data[c, h] * data[c, h], axis=0, keepdims=True)
        put_weights(h, pl.ds(0, src), data[0, h], data[1, h])
    data_norm = full_sum(data_norm)
    for load in loads[1::2]:
        load.wait()
    tile = 256
    for h in range(nf):
        for c in range(2):

            def flip(i, carry):
                cols = pl.ds(pl.multiple_of(i * tile, tile), tile)
                kern_t[c, h, cols, :] = kern[c, h, :, cols].T
                return carry

            lax.fori_loop(0, rec // tile, flip, 0)
    adjoint(0)
    pl.semaphore_wait(barrier, group - 1)
    exchange(image_out, image_in, 0, 0, 0)
    exchange(image_out, image_in, 0, 0, 1)

    norms = []
    for part in range(2):
        arrived(image_out, image_in, 0, 0, part)

        def keep_model(row, value):
            model[row] = value
            return value

        norms.append(window(0, part, keep_model))
        if part == 1:
            share(0, (data_norm, full_sum(norms[0] + norms[1])))
        exchange(spec_out, spec_in, 1, 0, part)

    square_data, square_model = collect(0, 2)
    beta0 = jnp.sqrt(square_data)
    size0 = jnp.sqrt(square_model)
    alpha0 = size0 / beta0
    for part in range(2):
        arrived(spec_out, spec_in, 1, 0, part)
    gain = 1.0 / size0
    back = alpha0 / beta0

    def first_resid(h, rows, got):
        real = got[:, :focal] * gain - back * data[0, h, rows, :]
        imag = got[:, focal:] * gain - back * data[1, h, rows, :]
        value = jnp.concatenate([real, imag], axis=1)
        resid[h, rows, :] = value
        return value

    resid_square = forward(0, first_resid)
    share(1, (resid_square,))

    for h in range(nf):
        put_weights(h, pl.ds(0, src), resid[h, :, :focal], resid[h, :, focal:])
    adjoint(1)
    exchange(image_out, image_in, 0, 1, 0)
    exchange(image_out, image_in, 0, 1, 1)

    (square1,) = collect(1, 1)
    beta1 = jnp.sqrt(square1)
    scale1 = 1.0 / beta1
    back1 = beta1 / size0
    norms = []
    for part in range(2):
        arrived(image_out, image_in, 0, 1, part)

        def subtract(row, value):
            value = value * scale1 - back1 * model[row]
            field[row] = value
            return value

        norms.append(window(1, part, subtract))
        if part == 1:
            share(2, (full_sum(norms[0] + norms[1]),))
        exchange(spec_out, spec_in, 1, 1, part)

    (square2,) = collect(2, 1)
    alpha1 = jnp.sqrt(square2)
    gain2 = 1.0 / alpha1
    back2 = alpha1 / beta1
    for part in range(2):
        arrived(spec_out, spec_in, 1, 1, part)

    def second_resid(h, rows, got):
        return got * gain2 - back2 * resid[h, rows, :]

    last_square = forward(1, second_resid)
    share(3, (last_square,))
    (square3,) = collect(3, 1)
    beta2 = jnp.sqrt(square3)
    rho1 = jnp.sqrt(alpha0 * alpha0 + beta1 * beta1)
    cosine = alpha0 / rho1
    sine = beta1 / rho1
    theta = sine * alpha1
    rhobar = -cosine * alpha1
    phi1 = cosine * beta0
    phibar = sine * beta0
    rho2 = jnp.sqrt(rhobar * rhobar + beta2 * beta2)
    phi2 = rhobar / rho2 * phibar
    step2 = phi2 / rho2
    on_field = step2 / alpha1
    on_model = (phi1 / rho1 - step2 * (theta / rho1)) / size0
    held = onset.shape[0]
    for row in range(held):
        out[pl.ds(row, samples, stride=held), :] = on_model * model[row] + on_field * field[row]

    for turn in range(2):
        for part in range(2):
            sent(image_out, 0, turn, part)
            sent(spec_out, 1, turn, part)
    for slot in range(4):
        rest = sums_in.at[slot, pl.ds(0, group - 1)]
        pltpu.make_async_copy(rest, rest, sum_send.at[slot]).wait()


def solution(mesh):
    group = mesh.shape["freq"]

    def shard(kernel, recorded, onset_time):
        nf, src, rec = kernel.shape[1:]
        held, focal = onset_time.shape
        bins = group * nf
        samples = 2 * bins
        forth = dft_tables(bins)
        moved = (2, 2, group, nf, 2 * HALF, focal)
        dma = pltpu.SemaphoreType.DMA
        x = pl.pallas_call(
            functools.partial(body, group),
            out_shape=jax.ShapeDtypeStruct((samples * held, focal), F32),
            in_specs=[
                pl.BlockSpec(memory_space=pl.ANY),
                pl.BlockSpec(memory_space=pl.ANY),
                pl.BlockSpec(memory_space=pltpu.VMEM),
                pl.BlockSpec(memory_space=pltpu.VMEM),
                pl.BlockSpec(memory_space=pltpu.VMEM),
            ],
            out_specs=pl.BlockSpec(memory_space=pltpu.VMEM),
            scratch_shapes=[
                pltpu.VMEM(kernel.shape, BF16),
                pltpu.VMEM((2, nf, rec, src), BF16),
                pltpu.VMEM(recorded.shape, F32),
                pltpu.VMEM((nf, src, 2 * focal), F32),
                pltpu.VMEM((nf, src + rec, 2 * focal), BF16),
                pltpu.VMEM((held, samples, focal), F32),
                pltpu.VMEM((held, samples, focal), F32),
                pltpu.VMEM(moved, BF16),
                pltpu.VMEM(moved, BF16),
                pltpu.VMEM(moved, BF16),
                pltpu.VMEM(moved, BF16),
                pltpu.VMEM((bins * 2 * HALF, focal), F32),
                pltpu.VMEM((4, 1, 128), F32),
                pltpu.VMEM((4, group, 1, 128), F32),
                dma((2, 2, nf)),
                dma((2, 2, 2)),
                dma((2, 2, 2)),
                dma((2, 2, 2)),
                dma((4,)),
                dma((4,)),
            ],
            compiler_params=pltpu.CompilerParams(
                collective_id=0, has_side_effects=True, vmem_limit_bytes=60 * MIB
            ),
        )(kernel, recorded, onset_time, jnp.asarray(forth), jnp.asarray(np.ascontiguousarray(forth.T)))
        return x.reshape(samples, held, focal)

    placed = (
        P(None, ("grp", "freq"), None, None),
        P(None, ("grp", "freq"), None, None),
        P(("grp", "freq"), None),
    )
    return jax.shard_map(
        shard, mesh=mesh, in_specs=placed, out_specs=P(None, ("grp", "freq"), None), check_vma=False
    )
```

time: 747 us -> 439 us (0.59); the launches traced: 739 us -> 439 us
  Pallas kernels: 0 us -> 436 us
  blocking collectives: 436 us -> 0 us
  waiting for transfers between devices: 209 us -> 0 us
  matrix products: 43.9 us -> 0 us
  starting transfers between devices: 15.9 us -> 0 us
  other arithmetic: 14.6 us -> 0 us
  local copies, waits for them, and re-layouts: 13.9 us -> 3.05 us
    pallas_call x0 -> x1, Pallas kernels: none -> 436 us  [shard(): pl.pallas_call(functools.partial(body, group), out_shape=jax.ShapeDtypeSt...]
    all_to_all x2 -> x0, blocking collectives: 259 us -> none  [apply_adjoint(): lax.all_to_all(image, FREQ, split_axis=2, concat_axis=1, tiled=True)]
    all_to_all x2 -> x0, waiting for transfers between devices: 209 us -> none  [body(): lax.all_to_all(spectrum, FREQ, split_axis=1, concat_axis=2, tiled=True)]
    psum x6 -> x0, blocking collectives: 178 us -> none  [by_axis(): return functools.reduce(lax.psum, axes, shard)]
    dot_general x24 -> x0, matrix products: 43.9 us -> none  [the longest x2 7.7 us: body(): jnp.einsum('ptx,pxi->pti', kernel_imaginary, solution_imaginary, preferre...]
    all_to_all x2 -> x0, starting transfers between devices: 15.9 us -> none  [body(): lax.all_to_all(spectrum, FREQ, split_axis=1, concat_axis=2, tiled=True)]
  transfers between devices with their start and end apart: 2 -> 0, of which waited for: 2 -> 0; matrix products, arithmetic and copies ran while one was open for 1% -> 0% of each run, Pallas kernels for 0% -> 0%
where the time goes in v1:
time: 439 us
  Pallas kernels  436 us (99%)
    pallas_call x1, Pallas kernels, shard(): pl.pallas_call(functools.partial(body, group), out_shape=jax.ShapeDtypeSt...  436 us

profile of v1, /device:TPU:37, one launch (start us, length us, event | category | flops | bytes accessed | tf_op | source)
XLA Modules:
  0.0 439.0 jit_solution(128872399303736264)
XLA Ops:
  0.0 436.0 %shard_map.55 = f32[4096,128]{1,0:T(8,128)} custom-call(bf16[2,2,1024,1024]{3,2,1,0:T(8,128)(2,1)} %kern_hbm.1, f32[2,2,1024,128]{3,2,1,0:T(8,128)} %data_hbm.1, s32[16,128]{1,0:T(8,128)} %onset.1, bf16[256,256]{1,0:T(8,128)(2,1)} %constant.4.clone.to_freq, bf16[256,256]{1,0:T(8,128)(2,1)} %constant.5.clone.to_time), custom_call_target="tpu_custom_call" | custom-call | tf_op jit(solution)/shard_map/pallas_call | solution.py:385
  436.0 3.0 copy.7

commit v2 on v1

v2 whole, which is shorter than its diff:
```python
import functools

import jax
import jax.numpy as jnp
import numpy as np
from jax import lax
from jax.experimental import pallas as pl
from jax.experimental.pallas import tpu as pltpu
from jax.sharding import PartitionSpec as P

CORES = 2
HALF = 8
MIB = 2**20
TEAMS = 4
TEAM_ORDER = (2, 1, 3, 0)
LIMIT = 42
MESH = pl.DeviceIdType.MESH
F32 = jnp.float32
BF16 = jnp.bfloat16


def dft_tables(bins):
    samples = 2 * bins
    phase = np.outer(np.arange(bins), np.arange(samples)) % samples * (np.pi / bins)
    scale = 1.0 / np.sqrt(bins)
    both = np.concatenate([np.cos(phase) * scale, -np.sin(phase) * scale], axis=0)
    return both.astype(jnp.bfloat16)


def dot(left, right):
    return jnp.dot(left, right, preferred_element_type=F32)


def body(
    group,
    kern_hbm,
    data_hbm,
    onset,
    to_freq,
    to_time,
    model_hbm,
    field_hbm,
    mix,
    kern,
    kern_t,
    data,
    resid,
    duals,
    weights,
    partial,
    model,
    field,
    image_out,
    image_in,
    spec_out,
    spec_in,
    wide,
    sums_out,
    sums_in,
    data_sem,
    kern_sem,
    send_sem,
    image_sem,
    spec_sem,
    own_sem,
    sum_send,
    sum_recv,
    save_sem,
):
    me = lax.axis_index("freq")
    chips = group // CORES
    chip = me // CORES
    core = lax.rem(me, CORES)
    nf = kern.shape[1]
    src = kern.shape[2]
    focal = onset.shape[1]
    held = onset.shape[0]
    bins = group * nf
    samples = 2 * bins
    team = group // TEAMS
    mine = me // team
    seat = lax.rem(me, team)
    block = team * held
    order = [lax.rem(mine + i, TEAMS) for i in TEAM_ORDER]

    def peer(chip_step, core_step):
        return lax.rem(chip + chip_step + chips, chips) * CORES + lax.rem(core + core_step, CORES)

    def for_peers(act):
        far = chips // 2
        for other in range(CORES):
            act(peer(far, other))

        def step(i, carry):
            d = far - 1 - i
            for other in range(CORES):
                act(peer(d, other))
                act(peer(-d, other))
            return carry

        lax.fori_loop(0, far - 1, step, 0)
        act(peer(0, 1))

    barrier = pltpu.get_barrier_semaphore()
    for_peers(
        lambda p: pl.semaphore_signal(barrier, inc=1, device_id={"freq": p}, device_id_type=MESH)
    )

    def cols_of(t):
        return pl.ds(pl.multiple_of(order[t] * block, block), block)

    def data_load(c, h):
        return pltpu.make_async_copy(data_hbm.at[c, h], data.at[c, h], data_sem.at[c, h])

    def kern_load(t, c, h):
        where = (c, h, slice(None), cols_of(t))
        return pltpu.make_async_copy(kern_hbm.at[where], kern.at[where], kern_sem.at[t, c, h])

    for h in range(nf):
        for c in range(2):
            data_load(c, h).start()
    for t in range(TEAMS):
        for h in range(nf):
            for c in range(2):
                kern_load(t, c, h).start()

    def remote(outgoing, incoming, kind, turn, part, recv, p):
        pltpu.make_async_remote_copy(
            src_ref=outgoing.at[turn, part, p],
            dst_ref=incoming.at[turn, part, me],
            send_sem=send_sem.at[kind, turn, part],
            recv_sem=recv,
            device_id={"freq": p},
            device_id_type=MESH,
        ).start()

    def own(outgoing, incoming, kind, turn, part):
        return pltpu.make_async_copy(
            outgoing.at[turn, part, me], incoming.at[turn, part, me], own_sem.at[kind, turn, part]
        )

    def send_image(turn, part, p):
        remote(image_out, image_in, 0, turn, part, image_sem.at[turn, part], p)

    def image_arrived(turn, part):
        rest = image_in.at[turn, part, pl.ds(0, group - 1)]
        pltpu.make_async_copy(rest, rest, image_sem.at[turn, part]).wait()
        own(image_out, image_in, 0, turn, part).wait()

    def send_spec(turn, part):
        for_peers(
            lambda p: remote(spec_out, spec_in, 1, turn, part, spec_sem.at[turn, part, mine], p)
        )
        own(spec_out, spec_in, 1, turn, part).start()

    def spec_arrived(turn, part, t):
        count = team - 1 if TEAM_ORDER[t] == 0 else team
        rest = spec_in.at[turn, part, pl.ds(0, count)]
        pltpu.make_async_copy(rest, rest, spec_sem.at[turn, part, order[t]]).wait()
        if TEAM_ORDER[t] == 0:
            own(spec_out, spec_in, 1, turn, part).wait()

    def sent(outgoing, kind, turn, part):
        rest = outgoing.at[turn, part, pl.ds(0, group - 1)]
        pltpu.make_async_copy(rest, rest, send_sem.at[kind, turn, part]).wait()

    lane = lax.broadcasted_iota(jnp.int32, (1, 128), 1)

    def row_of(values):
        row = jnp.zeros((1, 128), F32)
        for i, value in enumerate(values):
            row = jnp.where(lane == i, value, row)
        return row

    def share(slot, values):
        row = row_of(values)
        sums_out[slot] = row
        sums_in[slot, me] = row

        def push(p):
            pltpu.make_async_remote_copy(
                src_ref=sums_out.at[slot],
                dst_ref=sums_in.at[slot, me],
                send_sem=sum_send.at[slot],
                recv_sem=sum_recv.at[slot],
                device_id={"freq": p},
                device_id_type=MESH,
            ).start()

        for_peers(push)

    def collect(slot, count):
        rest = sums_in.at[slot, pl.ds(0, group - 1)]
        pltpu.make_async_copy(rest, rest, sum_recv.at[slot]).wait()
        total = jnp.sum(sums_in[slot], axis=0)
        return [jnp.sum(jnp.where(lane == i, total, 0.0), axis=1, keepdims=True) for i in range(count)]

    def full_sum(values):
        return jnp.sum(jnp.sum(values, axis=0, keepdims=True), axis=1, keepdims=True)

    def put_duals(h, rows, real, imag):
        low = pl.ds(pl.multiple_of(src + rows.start, 128), rows.size)
        duals[h, rows, :focal] = real.astype(BF16)
        duals[h, rows, focal:] = imag.astype(BF16)
        duals[h, low, :focal] = imag.astype(BF16)
        duals[h, low, focal:] = (-real).astype(BF16)

    tile = 256

    def adjoint(turn, t, ready):
        rows = cols_of(t)
        owner = order[t] * team
        for h in range(nf):
            ready(t, h)
            got = dot(kern_t[0, h, rows, :], duals[h, :src, :]) + dot(
                kern_t[1, h, rows, :], duals[h, src:, :]
            )
            real = got[:, :focal].reshape(team, 2, HALF, focal)
            imag = got[:, focal:].reshape(team, 2, HALF, focal)
            for part in range(2):
                image_out[turn, part, pl.ds(owner, team), h] = jnp.concatenate(
                    [real[:, part], imag[:, part]], axis=1
                ).astype(BF16)

    def send_team(turn, t):
        first = 1 if TEAM_ORDER[t] == 0 else 0

        def push(i, carry):
            send_image(turn, 0, order[t] * team + lax.rem(seat + i, team))
            return carry

        lax.fori_loop(first, team, push, 0)

    def send_rest(turn):
        own(image_out, image_in, 0, turn, 0).start()
        for_peers(lambda p: send_image(turn, 1, p))
        own(image_out, image_in, 0, turn, 1).start()

    def row_at(row):
        return pl.ds(row, samples, stride=held)

    def window(turn, part, combine):
        wide[...] = image_in[turn, part].astype(F32).reshape(bins * 2 * HALF, focal)
        norm = jnp.zeros((1, 2 * focal), F32)
        time = lax.broadcasted_iota(jnp.int32, (samples, focal), 0)
        for pair in range(HALF // 2):
            first, second = 2 * pair, 2 * pair + 1

            def column(r):
                return jnp.concatenate(
                    [
                        wide[pl.ds(r, bins, stride=2 * HALF), :],
                        wide[pl.ds(HALF + r, bins, stride=2 * HALF), :],
                    ],
                    axis=0,
                ).astype(BF16)

            timed = dot(to_time[...], jnp.concatenate([column(first), column(second)], axis=1))
            kept = []
            for i, r in enumerate((first, second)):
                row = part * HALF + r
                keep = time < onset[pl.ds(row, 1), :]
                value = jnp.where(keep, timed[:, i * focal : (i + 1) * focal], 0.0)
                kept.append(combine(row, value))
            kept = jnp.concatenate(kept, axis=1)
            norm = norm + jnp.sum(kept * kept, axis=0, keepdims=True)
            spec = dot(to_freq[...], kept.astype(BF16))
            for i, r in enumerate((first, second)):
                cols = slice(i * focal, (i + 1) * focal)
                wide[pl.ds(r, bins, stride=2 * HALF), :] = spec[:bins, cols]
                wide[pl.ds(HALF + r, bins, stride=2 * HALF), :] = spec[bins:, cols]
        spec_out[turn, part] = wide[...].reshape(group, nf, 2 * HALF, focal).astype(BF16)
        return norm

    def forward(turn, finish):
        norm = jnp.zeros((1, 2 * focal), F32)
        for t in range(TEAMS):
            for part in range(2):
                spec_arrived(turn, part, t)
            for h in range(nf):
                blocks = [
                    spec_in[turn, part, pl.ds(order[t] * team, team), h].astype(F32)
                    for part in range(2)
                ]
                real = jnp.concatenate([b[:, :HALF] for b in blocks], axis=1).reshape(block, focal)
                imag = jnp.concatenate([b[:, HALF:] for b in blocks], axis=1).reshape(block, focal)
                weights[h, 0, :, :focal] = real.astype(BF16)
                weights[h, 0, :, focal:] = imag.astype(BF16)
                weights[h, 1, :, :focal] = (-imag).astype(BF16)
                weights[h, 1, :, focal:] = real.astype(BF16)

                def step(i, norm):
                    rows = pl.ds(pl.multiple_of(i * tile, tile), tile)
                    got = dot(kern[0, h, rows, cols_of(t)], weights[h, 0]) + dot(
                        kern[1, h, rows, cols_of(t)], weights[h, 1]
                    )
                    if t > 0:
                        got = got + partial[h, rows, :]
                    if t < TEAMS - 1:
                        partial[h, rows, :] = got
                        return norm
                    value = finish(h, rows, got)
                    return norm + jnp.sum(value * value, axis=0, keepdims=True)

                norm = lax.fori_loop(0, src // tile, step, norm)
        return full_sum(norm)

    for h in range(nf):
        for c in range(2):
            data_load(c, h).wait()
        put_duals(h, pl.ds(0, src), data[0, h], data[1, h])

    def turn_block(t, h):
        for c in range(2):
            kern_load(t, c, h).wait()

            def flip(i, carry):
                at = pl.ds(pl.multiple_of(i * tile, tile), tile)
                kern_t[c, h, cols_of(t), at] = kern[c, h, at, cols_of(t)].T
                return carry

            lax.fori_loop(0, src // tile, flip, 0)

    for t in range(TEAMS):
        adjoint(0, t, turn_block)
        if t == 0:
            pl.semaphore_wait(barrier, group - 1)
        send_team(0, t)
    send_rest(0)
    data_norm = jnp.zeros((1, focal), F32)
    for h in range(nf):
        for c in range(2):
            data_norm = data_norm + jnp.sum(data[c, h] * data[c, h], axis=0, keepdims=True)
    data_norm = full_sum(data_norm)

    norms = []
    for part in range(2):
        image_arrived(0, part)

        def keep_model(row, value):
            model[row_at(row), :] = value
            return value

        norms.append(window(0, part, keep_model))
        if part == 1:
            share(0, (data_norm, full_sum(norms[0] + norms[1])))
        send_spec(0, part)
    save_model = pltpu.make_async_copy(model, model_hbm, save_sem.at[0])
    save_model.start()

    square_data, square_model = collect(0, 2)
    beta0 = jnp.sqrt(square_data)
    size0 = jnp.sqrt(square_model)
    alpha0 = size0 / beta0
    gain = 1.0 / size0
    back = alpha0 / beta0

    def first_resid(h, rows, got):
        real = got[:, :focal] * gain - back * data[0, h, rows, :]
        imag = got[:, focal:] * gain - back * data[1, h, rows, :]
        put_duals(h, rows, real, imag)
        value = jnp.concatenate([real, imag], axis=1)
        resid[h, rows, :] = value
        return value

    resid_square = forward(0, first_resid)
    share(1, (resid_square,))
    for t in range(TEAMS):
        adjoint(1, t, lambda t, h: None)
        send_team(1, t)
    send_rest(1)

    (square1,) = collect(1, 1)
    beta1 = jnp.sqrt(square1)
    scale1 = 1.0 / beta1
    back1 = beta1 / size0
    norms = []
    for part in range(2):
        image_arrived(1, part)

        def subtract(row, value):
            value = value * scale1 - back1 * model[row_at(row), :]
            field[row_at(row), :] = value
            return value

        norms.append(window(1, part, subtract))
        if part == 1:
            share(2, (full_sum(norms[0] + norms[1]),))
        send_spec(1, part)
    save_field = pltpu.make_async_copy(field, field_hbm, save_sem.at[1])
    save_field.start()

    (square2,) = collect(2, 1)
    alpha1 = jnp.sqrt(square2)
    gain2 = 1.0 / alpha1
    back2 = alpha1 / beta1

    def second_resid(h, rows, got):
        return got * gain2 - back2 * resid[h, rows, :]

    last_square = forward(1, second_resid)
    share(3, (last_square,))
    save_model.wait()
    save_field.wait()
    for turn in range(2):
        for part in range(2):
            sent(image_out, 0, turn, part)
            sent(spec_out, 1, turn, part)
    for slot in range(4):
        rest = sums_in.at[slot, pl.ds(0, group - 1)]
        pltpu.make_async_copy(rest, rest, sum_send.at[slot]).wait()
    (square3,) = collect(3, 1)
    beta2 = jnp.sqrt(square3)
    rho1 = jnp.sqrt(alpha0 * alpha0 + beta1 * beta1)
    cosine = alpha0 / rho1
    sine = beta1 / rho1
    theta = sine * alpha1
    rhobar = -cosine * alpha1
    phi1 = cosine * beta0
    phibar = sine * beta0
    rho2 = jnp.sqrt(rhobar * rhobar + beta2 * beta2)
    phi2 = rhobar / rho2 * phibar
    step2 = phi2 / rho2
    on_field = step2 / alpha1
    on_model = (phi1 / rho1 - step2 * (theta / rho1)) / size0
    mix[0:1, :] = jnp.broadcast_to(on_model, (1, focal))
    mix[1:2, :] = jnp.broadcast_to(on_field, (1, focal))


def solution(mesh):
    group = mesh.shape["freq"]

    def shard(kernel, recorded, onset_time):
        nf, src, rec = kernel.shape[1:]
        held, focal = onset_time.shape
        bins = group * nf
        samples = 2 * bins
        forth = dft_tables(bins)
        moved = (2, 2, group, nf, 2 * HALF, focal)
        flat = (samples * held, focal)
        dma = pltpu.SemaphoreType.DMA
        vmem = pl.BlockSpec(memory_space=pltpu.VMEM)
        anywhere = pl.BlockSpec(memory_space=pl.ANY)
        model, field, mix = pl.pallas_call(
            functools.partial(body, group),
            out_shape=(
                jax.ShapeDtypeStruct(flat, F32),
                jax.ShapeDtypeStruct(flat, F32),
                jax.ShapeDtypeStruct((2, focal), F32),
            ),
            in_specs=[anywhere, anywhere, vmem, vmem, vmem],
            out_specs=(anywhere, anywhere, vmem),
            scratch_shapes=[
                pltpu.VMEM(kernel.shape, BF16),
                pltpu.VMEM((2, nf, rec, src), BF16),
                pltpu.VMEM(recorded.shape, F32),
                pltpu.VMEM((nf, src, 2 * focal), F32),
                pltpu.VMEM((nf, 2 * src, 2 * focal), BF16),
                pltpu.VMEM((nf, 2, rec // TEAMS, 2 * focal), BF16),
                pltpu.VMEM((nf, src, 2 * focal), F32),
                pltpu.VMEM(flat, F32),
                pltpu.VMEM(flat, F32),
                pltpu.VMEM(moved, BF16),
                pltpu.VMEM(moved, BF16),
                pltpu.VMEM(moved, BF16),
                pltpu.VMEM(moved, BF16),
                pltpu.VMEM((bins * 2 * HALF, focal), F32),
                pltpu.VMEM((4, 1, 128), F32),
                pltpu.VMEM((4, group, 1, 128), F32),
                dma((2, nf)),
                dma((TEAMS, 2, nf)),
                dma((2, 2, 2)),
                dma((2, 2)),
                dma((2, 2, TEAMS)),
                dma((2, 2, 2)),
                dma((4,)),
                dma((4,)),
                dma((2,)),
            ],
            compiler_params=pltpu.CompilerParams(
                collective_id=0, has_side_effects=True, vmem_limit_bytes=LIMIT * MIB
            ),
        )(kernel, recorded, onset_time, jnp.asarray(forth), jnp.asarray(np.ascontiguousarray(forth.T)))
        x = mix[0:1] * model + mix[1:2] * field
        return x.reshape(samples, held, focal)

    placed = (
        P(None, ("grp", "freq"), None, None),
        P(None, ("grp", "freq"), None, None),
        P(("grp", "freq"), None),
    )
    return jax.shard_map(
        shard, mesh=mesh, in_specs=placed, out_specs=P(None, ("grp", "freq"), None), check_vma=False
    )
```

time: 439 us -> 434 us (0.989)
  Pallas kernels: 436 us -> 428 us
    pallas_call x1, Pallas kernels: 436 us -> 428 us  [shard(): pl.pallas_call(functools.partial(body, group), out_shape=(jax.ShapeDtypeS...]
where the time goes in v2:
time: 434 us; the launch traced here: 433 us
  Pallas kernels  428 us (99%)
    pallas_call x1, Pallas kernels, shard(): pl.pallas_call(functools.partial(body, group), out_shape=(jax.ShapeDtypeS...  428 us

profile of v2, /device:TPU:37, one launch (start us, length us, event | category | flops | bytes accessed | tf_op | source)
XLA Modules:
  0.0 433.4 jit_solution(10393954047552332308)
XLA Ops:
  0.0 0.0 copy-start
  0.0 1.6 copy-done
  1.6 0.0 copy-start.1
  1.6 0.9 copy-done.1
  2.5 0.0 copy-start.2
  2.5 0.9 copy-done.2
  3.4 0.0 copy-start.3
  3.4 0.7 copy-done.3
  4.1 427.7 %shard_map.55 = (f32[4096,128]{1,0:T(8,128)S(1)}, f32[4096,128]{1,0:T(8,128)S(1)}, f32[2,128]{1,0:T(2,128)S(1)}) custom-call(bf16[2,2,1024,1024]{3,2,1,0:T(8,128)(2,1)} %kern_hbm.1, f32[2,2,1024,128]{3,2,1,0:T(8,128)S(1)} %copy-done, s32[16,128]{1,0:T(8,128)S(1)} %copy-done.3, bf16[256,256]{1,0:T(8,128)(2,1)S(1)} %copy-done.2, bf16[256,256]{1,0:T(8,128)(2,1)S(1)} %copy-done.1), custom_call_target="tpu_custom_call" | custom-call | tf_op jit(solution)/shard_map/pallas_call | solution.py:444
  431.8 1.5 multiply_add_fusion
  (1 shorter events, 0.0 us)
Async XLA Ops:
  0.0 1.6 copy-start
  1.6 0.9 copy-start.1
  2.5 0.9 copy-start.2
  3.4 0.7 copy-start.3

commit v3 on v2

--- a/solution.py
+++ b/solution.py
@@ -13,7 +13,9 @@
 MIB = 2**20
 TEAMS = 4
 TEAM_ORDER = (2, 1, 3, 0)
-LIMIT = 42
+LIMIT = 58
+TALL = 512
+LAST = 3
 MESH = pl.DeviceIdType.MESH
 F32 = jnp.float32
 BF16 = jnp.bfloat16
@@ -35,12 +37,16 @@
     group,
     kern_hbm,
     data_hbm,
+    onset_hbm,
+    to_freq_hbm,
+    to_time_hbm,
+    model_hbm,
+    field_hbm,
+    on_model,
+    on_field,
     onset,
     to_freq,
     to_time,
-    model_hbm,
-    field_hbm,
-    mix,
     kern,
     kern_t,
     data,
@@ -55,14 +61,20 @@
     spec_out,
     spec_in,
     wide,
+    sums_own,
+    sums_mate,
     sums_out,
     sums_in,
+    last_in,
+    small_sem,
     data_sem,
     kern_sem,
     send_sem,
     image_sem,
     spec_sem,
     own_sem,
+    mate_send,
+    mate_recv,
     sum_send,
     sum_recv,
     save_sem,
@@ -73,8 +85,7 @@
     core = lax.rem(me, CORES)
     nf = kern.shape[1]
     src = kern.shape[2]
-    focal = onset.shape[1]
-    held = onset.shape[0]
+    held, focal = onset.shape
     bins = group * nf
     samples = 2 * bins
     team = group // TEAMS
@@ -123,6 +134,14 @@
         for h in range(nf):
             for c in range(2):
                 kern_load(t, c, h).start()
+    small = [
+        pltpu.make_async_copy(source, target, small_sem.at[i])
+        for i, (source, target) in enumerate(
+            ((onset_hbm, onset), (to_freq_hbm, to_freq), (to_time_hbm, to_time))
+        )
+    ]
+    for load in small:
+        load.start()
 
     def remote(outgoing, incoming, kind, turn, part, recv, p):
         pltpu.make_async_remote_copy(
@@ -172,26 +191,75 @@
             row = jnp.where(lane == i, value, row)
         return row
 
+    def mate_copy(slot):
+        return pltpu.make_async_remote_copy(
+            src_ref=sums_own.at[slot],
+            dst_ref=sums_mate.at[slot],
+            send_sem=mate_send.at[slot],
+            recv_sem=mate_recv.at[slot],
+            device_id={"freq": peer(0, 1)},
+            device_id_type=MESH,
+        )
+
     def share(slot, values):
-        row = row_of(values)
+        sums_own[slot] = row_of(values)
+        mate_copy(slot).start()
+
+    def relay(slot):
+        mate_copy(slot).wait()
+        row = sums_own[slot] + sums_mate[slot]
         sums_out[slot] = row
-        sums_in[slot, me] = row
+        sums_in[slot, chip] = row
 
         def push(p):
             pltpu.make_async_remote_copy(
                 src_ref=sums_out.at[slot],
-                dst_ref=sums_in.at[slot, me],
+                dst_ref=sums_in.at[slot, chip],
                 send_sem=sum_send.at[slot],
                 recv_sem=sum_recv.at[slot],
                 device_id={"freq": p},
                 device_id_type=MESH,
             ).start()
 
+        push(peer(chips // 2, 0))
+
+        def step(i, carry):
+            d = chips // 2 - 1 - i
+            push(peer(d, 0))
+            push(peer(-d, 0))
+            return carry
+
+        lax.fori_loop(0, chips // 2 - 1, step, 0)
+
+    def share_last(slot, value):
+        row = row_of((value,))
+        sums_out[slot] = row
+        last_in[me] = row
+
+        def push(p):
+            pltpu.make_async_remote_copy(
+                src_ref=sums_out.at[slot],
+                dst_ref=last_in.at[me],
+                send_sem=sum_send.at[slot],
+                recv_sem=sum_recv.at[slot],
+                device_id={"freq": p},
+                device_id_type=MESH,
+            ).start()
+
         for_peers(push)
 
+    def collect_last(slot):
+        sums_wait(slot, sum_recv)
+        total = jnp.sum(last_in[...], axis=0)
+        return jnp.sum(jnp.where(lane == 0, total, 0.0), axis=1, keepdims=True)
+
+    def sums_wait(slot, sem):
+        last = slot == LAST
+        rest = last_in.at[pl.ds(0, group - 1)] if last else sums_in.at[slot, pl.ds(0, chips - 1)]
+        pltpu.make_async_copy(rest, rest, sem.at[slot]).wait()
+
     def collect(slot, count):
-        rest = sums_in.at[slot, pl.ds(0, group - 1)]
-        pltpu.make_async_copy(rest, rest, sum_recv.at[slot]).wait()
+        sums_wait(slot, sum_recv)
         total = jnp.sum(sums_in[slot], axis=0)
         return [jnp.sum(jnp.where(lane == i, total, 0.0), axis=1, keepdims=True) for i in range(count)]
 
@@ -290,7 +358,7 @@
                 weights[h, 1, :, focal:] = real.astype(BF16)
 
                 def step(i, norm):
-                    rows = pl.ds(pl.multiple_of(i * tile, tile), tile)
+                    rows = pl.ds(pl.multiple_of(i * TALL, TALL), TALL)
                     got = dot(kern[0, h, rows, cols_of(t)], weights[h, 0]) + dot(
                         kern[1, h, rows, cols_of(t)], weights[h, 1]
                     )
@@ -302,7 +370,7 @@
                     value = finish(h, rows, got)
                     return norm + jnp.sum(value * value, axis=0, keepdims=True)
 
-                norm = lax.fori_loop(0, src // tile, step, norm)
+                norm = lax.fori_loop(0, src // TALL, step, norm)
         return full_sum(norm)
 
     for h in range(nf):
@@ -333,6 +401,8 @@
             data_norm = data_norm + jnp.sum(data[c, h] * data[c, h], axis=0, keepdims=True)
     data_norm = full_sum(data_norm)
 
+    for load in small:
+        load.wait()
     norms = []
     for part in range(2):
         image_arrived(0, part)
@@ -344,6 +414,7 @@
         norms.append(window(0, part, keep_model))
         if part == 1:
             share(0, (data_norm, full_sum(norms[0] + norms[1])))
+            relay(0)
         send_spec(0, part)
     save_model = pltpu.make_async_copy(model, model_hbm, save_sem.at[0])
     save_model.start()
@@ -368,6 +439,8 @@
     for t in range(TEAMS):
         adjoint(1, t, lambda t, h: None)
         send_team(1, t)
+        if t == 0:
+            relay(1)
     send_rest(1)
 
     (square1,) = collect(1, 1)
@@ -386,6 +459,7 @@
         norms.append(window(1, part, subtract))
         if part == 1:
             share(2, (full_sum(norms[0] + norms[1]),))
+            relay(2)
         send_spec(1, part)
     save_field = pltpu.make_async_copy(field, field_hbm, save_sem.at[1])
     save_field.start()
@@ -399,18 +473,16 @@
         return got * gain2 - back2 * resid[h, rows, :]
 
     last_square = forward(1, second_resid)
-    share(3, (last_square,))
+    share_last(LAST, last_square)
     save_model.wait()
     save_field.wait()
     for turn in range(2):
         for part in range(2):
             sent(image_out, 0, turn, part)
             sent(spec_out, 1, turn, part)
-    for slot in range(4):
-        rest = sums_in.at[slot, pl.ds(0, group - 1)]
-        pltpu.make_async_copy(rest, rest, sum_send.at[slot]).wait()
-    (square3,) = collect(3, 1)
-    beta2 = jnp.sqrt(square3)
+    for slot in range(LAST + 1):
+        sums_wait(slot, sum_send)
+    beta2 = jnp.sqrt(collect_last(LAST))
     rho1 = jnp.sqrt(alpha0 * alpha0 + beta1 * beta1)
     cosine = alpha0 / rho1
     sine = beta1 / rho1
@@ -421,10 +493,10 @@
     rho2 = jnp.sqrt(rhobar * rhobar + beta2 * beta2)
     phi2 = rhobar / rho2 * phibar
     step2 = phi2 / rho2
-    on_field = step2 / alpha1
-    on_model = (phi1 / rho1 - step2 * (theta / rho1)) / size0
-    mix[0:1, :] = jnp.broadcast_to(on_model, (1, focal))
-    mix[1:2, :] = jnp.broadcast_to(on_field, (1, focal))
+    on_field[...] = jnp.broadcast_to(step2 / alpha1, on_field.shape)
+    on_model[...] = jnp.broadcast_to(
+        (phi1 / rho1 - step2 * (theta / rho1)) / size0, on_model.shape
+    )
 
 
 def solution(mesh):
@@ -439,18 +511,22 @@
         moved = (2, 2, group, nf, 2 * HALF, focal)
         flat = (samples * held, focal)
         dma = pltpu.SemaphoreType.DMA
+        anywhere = pl.BlockSpec(memory_space=pl.ANY)
         vmem = pl.BlockSpec(memory_space=pltpu.VMEM)
-        anywhere = pl.BlockSpec(memory_space=pl.ANY)
-        model, field, mix = pl.pallas_call(
+        model, field, on_model, on_field = pl.pallas_call(
             functools.partial(body, group),
             out_shape=(
-                jax.ShapeDtypeStruct(flat, F32),
-                jax.ShapeDtypeStruct(flat, F32),
-                jax.ShapeDtypeStruct((2, focal), F32),
+                pltpu.VMEM(flat, F32),
+                pltpu.VMEM(flat, F32),
+                pltpu.VMEM((1, focal), F32),
+                pltpu.VMEM((1, focal), F32),
             ),
-            in_specs=[anywhere, anywhere, vmem, vmem, vmem],
-            out_specs=(anywhere, anywhere, vmem),
+            in_specs=[pl.BlockSpec(memory_space=pltpu.HBM)] * 5,
+            out_specs=(anywhere, anywhere, vmem, vmem),
             scratch_shapes=[
+                pltpu.VMEM(onset_time.shape, jnp.int32),
+                pltpu.VMEM(forth.shape, BF16),
+                pltpu.VMEM(forth.shape[::-1], BF16),
                 pltpu.VMEM(kernel.shape, BF16),
                 pltpu.VMEM((2, nf, rec, src), BF16),
                 pltpu.VMEM(recorded.shape, F32),
@@ -465,23 +541,29 @@
                 pltpu.VMEM(moved, BF16),
                 pltpu.VMEM(moved, BF16),
                 pltpu.VMEM((bins * 2 * HALF, focal), F32),
-                pltpu.VMEM((4, 1, 128), F32),
-                pltpu.VMEM((4, group, 1, 128), F32),
+                pltpu.VMEM((LAST, 1, 128), F32),
+                pltpu.VMEM((LAST, 1, 128), F32),
+                pltpu.VMEM((LAST + 1, 1, 128), F32),
+                pltpu.VMEM((LAST, group // CORES, 1, 128), F32),
+                pltpu.VMEM((group, 1, 128), F32),
+                dma((3,)),
                 dma((2, nf)),
                 dma((TEAMS, 2, nf)),
                 dma((2, 2, 2)),
                 dma((2, 2)),
                 dma((2, 2, TEAMS)),
                 dma((2, 2, 2)),
-                dma((4,)),
-                dma((4,)),
+                dma((LAST,)),
+                dma((LAST,)),
+                dma((LAST + 1,)),
+                dma((LAST + 1,)),
                 dma((2,)),
             ],
             compiler_params=pltpu.CompilerParams(
                 collective_id=0, has_side_effects=True, vmem_limit_bytes=LIMIT * MIB
             ),
         )(kernel, recorded, onset_time, jnp.asarray(forth), jnp.asarray(np.ascontiguousarray(forth.T)))
-        x = mix[0:1] * model + mix[1:2] * field
+        x = on_model * model + on_field * field
         return x.reshape(samples, held, focal)
 
     placed = (

time: 434 us -> 423 us (0.975)
  Pallas kernels: 428 us -> 421 us
    pallas_call x1, Pallas kernels: 428 us -> 421 us  [shard(): pl.pallas_call(functools.partial(body, group), out_shape=(pltpu.VMEM(flat...]
where the time goes in v3:
time: 423 us
  Pallas kernels  421 us (100%)
    pallas_call x1, Pallas kernels, shard(): pl.pallas_call(functools.partial(body, group), out_shape=(pltpu.VMEM(flat...  421 us

profile of v3, /device:TPU:37, one launch (start us, length us, event | category | flops | bytes accessed | tf_op | source)
XLA Modules:
  0.0 422.9 jit_solution(1084871346670683319)
XLA Ops:
  0.0 421.4 %shard_map.55 = (f32[4096,128]{1,0:T(8,128)S(1)}, f32[4096,128]{1,0:T(8,128)S(1)}, f32[1,128]{1,0:T(1,128)S(1)}, f32[1,128]{1,0:T(1,128)S(1)}) custom-call(bf16[2,2,1024,1024]{3,2,1,0:T(8,128)(2,1)} %kern_hbm.1, f32[2,2,1024,128]{3,2,1,0:T(8,128)} %data_hbm.1, s32[16,128]{1,0:T(8,128)} %onset_hbm.1, bf16[256,256]{1,0:T(8,128)(2,1)} %constant.4.clone.to_freq_hbm, ...), custom_call_target="tpu_custom_call" | custom-call | tf_op jit(solution)/shard_map/pallas_call | solution.py:516
  421.4 1.5 multiply_add_fusion

commit v4 on v3

--- a/solution.py
+++ b/solution.py
@@ -112,25 +112,27 @@
         lax.fori_loop(0, far - 1, step, 0)
         act(peer(0, 1))
 
+    def cols_of(t):
+        return pl.ds(pl.multiple_of(order[t] * block, block), block)
+
+    def data_load(c, h):
+        return pltpu.make_async_copy(data_hbm.at[c, h], data.at[c, h], data_sem.at[c, h])
+
+    def kern_load(t, c, h):
+        where = (c, h, slice(None), cols_of(t))
+        return pltpu.make_async_copy(kern_hbm.at[where], kern.at[where], kern_sem.at[t, c, h])
+
+    for h in range(nf):
+        for c in range(2):
+            data_load(c, h).start()
+    for h in range(nf):
+        for c in range(2):
+            kern_load(0, c, h).start()
     barrier = pltpu.get_barrier_semaphore()
     for_peers(
         lambda p: pl.semaphore_signal(barrier, inc=1, device_id={"freq": p}, device_id_type=MESH)
     )
-
-    def cols_of(t):
-        return pl.ds(pl.multiple_of(order[t] * block, block), block)
-
-    def data_load(c, h):
-        return pltpu.make_async_copy(data_hbm.at[c, h], data.at[c, h], data_sem.at[c, h])
-
-    def kern_load(t, c, h):
-        where = (c, h, slice(None), cols_of(t))
-        return pltpu.make_async_copy(kern_hbm.at[where], kern.at[where], kern_sem.at[t, c, h])
-
-    for h in range(nf):
-        for c in range(2):
-            data_load(c, h).start()
-    for t in range(TEAMS):
+    for t in range(1, TEAMS):
         for h in range(nf):
             for c in range(2):
                 kern_load(t, c, h).start()
@@ -191,45 +193,38 @@
             row = jnp.where(lane == i, value, row)
         return row
 
-    def mate_copy(slot):
+    def mate_copy(stage, slot):
         return pltpu.make_async_remote_copy(
-            src_ref=sums_own.at[slot],
-            dst_ref=sums_mate.at[slot],
-            send_sem=mate_send.at[slot],
-            recv_sem=mate_recv.at[slot],
+            src_ref=sums_own.at[stage, slot],
+            dst_ref=sums_mate.at[stage, slot],
+            send_sem=mate_send.at[stage, slot],
+            recv_sem=mate_recv.at[stage, slot],
             device_id={"freq": peer(0, 1)},
             device_id_type=MESH,
         )
 
     def share(slot, values):
-        sums_own[slot] = row_of(values)
-        mate_copy(slot).start()
+        sums_own[0, slot] = row_of(values)
+        mate_copy(0, slot).start()
+
+    far = chips // 2
 
     def relay(slot):
-        mate_copy(slot).wait()
-        row = sums_own[slot] + sums_mate[slot]
-        sums_out[slot] = row
-        sums_in[slot, chip] = row
-
-        def push(p):
+        mate_copy(0, slot).wait()
+        sums_out[slot] = sums_own[0, slot] + sums_mate[0, slot]
+
+        def step(i, carry):
             pltpu.make_async_remote_copy(
                 src_ref=sums_out.at[slot],
-                dst_ref=sums_in.at[slot, chip],
+                dst_ref=sums_in.at[slot, i],
                 send_sem=sum_send.at[slot],
                 recv_sem=sum_recv.at[slot],
-                device_id={"freq": p},
+                device_id={"freq": peer((far - i) * (1 - 2 * core), 0)},
                 device_id_type=MESH,
             ).start()
-
-        push(peer(chips // 2, 0))
-
-        def step(i, carry):
-            d = chips // 2 - 1 - i
-            push(peer(d, 0))
-            push(peer(-d, 0))
             return carry
 
-        lax.fori_loop(0, chips // 2 - 1, step, 0)
+        lax.fori_loop(0, far, step, 0)
 
     def share_last(slot, value):
         row = row_of((value,))
@@ -255,12 +250,16 @@
 
     def sums_wait(slot, sem):
         last = slot == LAST
-        rest = last_in.at[pl.ds(0, group - 1)] if last else sums_in.at[slot, pl.ds(0, chips - 1)]
+        rest = last_in.at[pl.ds(0, group - 1)] if last else sums_in.at[slot]
         pltpu.make_async_copy(rest, rest, sem.at[slot]).wait()
 
     def collect(slot, count):
         sums_wait(slot, sum_recv)
-        total = jnp.sum(sums_in[slot], axis=0)
+        once = (1 - core).astype(F32) * (sums_in[slot, 0] + sums_out[slot])
+        sums_own[1, slot] = once + jnp.sum(sums_in[slot, 1:far], axis=0)
+        mate_copy(1, slot).start()
+        mate_copy(1, slot).wait()
+        total = sums_own[1, slot] + sums_mate[1, slot]
         return [jnp.sum(jnp.where(lane == i, total, 0.0), axis=1, keepdims=True) for i in range(count)]
 
     def full_sum(values):
@@ -541,10 +540,10 @@
                 pltpu.VMEM(moved, BF16),
                 pltpu.VMEM(moved, BF16),
                 pltpu.VMEM((bins * 2 * HALF, focal), F32),
-                pltpu.VMEM((LAST, 1, 128), F32),
-                pltpu.VMEM((LAST, 1, 128), F32),
+                pltpu.VMEM((2, LAST, 1, 128), F32),
+                pltpu.VMEM((2, LAST, 1, 128), F32),
                 pltpu.VMEM((LAST + 1, 1, 128), F32),
-                pltpu.VMEM((LAST, group // CORES, 1, 128), F32),
+                pltpu.VMEM((LAST, group // CORES // 2, 1, 128), F32),
                 pltpu.VMEM((group, 1, 128), F32),
                 dma((3,)),
                 dma((2, nf)),
@@ -553,8 +552,8 @@
                 dma((2, 2)),
                 dma((2, 2, TEAMS)),
                 dma((2, 2, 2)),
-                dma((LAST,)),
-                dma((LAST,)),
+                dma((2, LAST)),
+                dma((2, LAST)),
                 dma((LAST + 1,)),
                 dma((LAST + 1,)),
                 dma((2,)),

time: 423 us -> 420 us (level)
  no operation moved by 1% of the time
where the time goes in v4:
time: 420 us
  Pallas kernels  419 us (100%)
    pallas_call x1, Pallas kernels, shard(): pl.pallas_call(functools.partial(body, group), out_shape=(pltpu.VMEM(flat...  419 us

profile of v4, /device:TPU:37, one launch (start us, length us, event | category | flops | bytes accessed | tf_op | source)
XLA Modules:
  0.0 420.2 jit_solution(8816685187891625294)
XLA Ops:
  0.0 418.7 %shard_map.55 = (f32[4096,128]{1,0:T(8,128)S(1)}, f32[4096,128]{1,0:T(8,128)S(1)}, f32[1,128]{1,0:T(1,128)S(1)}, f32[1,128]{1,0:T(1,128)S(1)}) custom-call(bf16[2,2,1024,1024]{3,2,1,0:T(8,128)(2,1)} %kern_hbm.1, f32[2,2,1024,128]{3,2,1,0:T(8,128)} %data_hbm.1, s32[16,128]{1,0:T(8,128)} %onset_hbm.1, bf16[256,256]{1,0:T(8,128)(2,1)} %constant.4.clone.to_freq_hbm, ...), custom_call_target="tpu_custom_call" | custom-call | tf_op jit(solution)/shard_map/pallas_call | solution.py:515
  418.7 1.5 multiply_add_fusion
